TPU v7x, 128 devices: a whole 4x4x4 slice. The times are simulated.
128 devices in a mesh: blk: 64 (over z_lo, x, y, core), grp: 2 (over z_hi).
Axes of the slice: x: 4, y: 4, z: 4 (z_hi: 2, z_lo: 2; z = z_hi * 2 + z_lo), core: 2. Of those that a mesh axis runs over, the one named last changes fastest.
Arguments:
- returns: float32 [512, 32768], P(None, ('blk', 'grp')), may hold values from -200 to 200
Outputs:
- correlation: bfloat16 [32768, 32768], P(('blk', 'grp'))
All inputs are finite; a program needn't handle non-finite values.
Results may differ from a plain program's by a relative error of at most 0.0034.
Values may be sent and summed in bfloat16 or wider, within the bound.
A program may use at most 128 MiB of HBM per device.

v0:
```python
import math

import jax
import jax.numpy as jnp
from jax import lax
from jax.sharding import Mesh
from jax.sharding import PartitionSpec as P

BLK_GRP = ("blk_0", "blk_1", "blk_2", "blk_3", "grp")


def by_axis(array, axes):
    for axis in axes:
        array = lax.psum(array, axis)
    return array


def gram_tile(first, second):
    return lax.dot_general(
        first, second, (((0,), (0,)), ((), ())), preferred_element_type=jnp.float32
    )


def shards(returns):
    bar_count = returns.shape[0]
    series_dev = returns.shape[1]
    devices = lax.axis_size(BLK_GRP)
    my_index = lax.axis_index(BLK_GRP)
    summed = by_axis(jnp.sum(returns, axis=1), BLK_GRP)
    market = summed / (series_dev * devices)
    excess = returns - market[:, None]
    deviation = excess - jnp.mean(excess, axis=0, keepdims=True)
    inverse = lax.rsqrt(jnp.mean(deviation * deviation, axis=0, keepdims=True) + 1e-06) / math.sqrt(
        bar_count
    )
    zscores = (deviation * inverse).astype(jnp.bfloat16)
    piece = lax.all_gather(zscores, BLK_GRP, axis=1, tiled=True)
    products = gram_tile(zscores, piece)
    column_block = jnp.arange(piece.shape[1], dtype=jnp.int32) // series_dev
    return jnp.where(column_block[None, :] >= my_index, products, jnp.float32(0.0)).astype(
        jnp.bfloat16
    )


def solution(mesh):
    split = Mesh(
        mesh.devices.reshape(2, 4, 4, 2, mesh.shape["grp"]),
        ("blk_0", "blk_1", "blk_2", "blk_3", "grp"),
    )
    in_specs = (P(None, BLK_GRP),)
    out_specs = P(BLK_GRP, None)
    return jax.shard_map(
        shards, mesh=split, in_specs=in_specs, out_specs=out_specs, check_vma=False
    )
```

profile of v0, /device:TPU:1, one launch (start us, length us, event | category | flops | bytes accessed | tf_op | source)
XLA Modules:
  0.0 429.9 jit_solution(4869989052520204716)
XLA Ops:
  6.5 0.0 all-gather.2.cloned.1.call-start
  6.5 1.2 reduce_sum.27
  7.7 4.8 %psum.35 = f32[512]{0:T(512)S(1)} all-reduce(f32[512]{0:T(512)S(1)} %reduce_sum.27), channel_id=1, replica_groups=mesh['blk_0'=2,'blk_1'=4,'blk_2'=4,'blk_3'=2,'grp'=2] {'blk_0'}, use_global_device_ids=true, to_apply=%region_1.0 | all-reduce | flops 512 | bytes 4096 | tf_op jit(solution)/shard_map/psum | solution.py:14
  12.5 8.4 %psum.36 = f32[512]{0:T(512)S(1)} all-reduce(f32[512]{0:T(512)S(1)} %psum.35), channel_id=1, replica_groups=mesh['blk_0'=2,'blk_1'=4,'blk_2'=4,'blk_3'=2,'grp'=2] {'blk_1'}, use_global_device_ids=true, to_apply=%region_2.0 | all-reduce | flops 512 | bytes 4096 | tf_op jit(solution)/shard_map/psum | solution.py:14
  20.9 8.7 %psum.37 = f32[512]{0:T(512)S(1)} all-reduce(f32[512]{0:T(512)S(1)} %psum.36), channel_id=1, replica_groups=mesh['blk_0'=2,'blk_1'=4,'blk_2'=4,'blk_3'=2,'grp'=2] {'blk_2'}, use_global_device_ids=true, to_apply=%region_3.0 | all-reduce | flops 512 | bytes 4096 | tf_op jit(solution)/shard_map/psum | solution.py:14
  29.6 7.8 %psum.38 = f32[512]{0:T(512)S(1)} all-reduce(f32[512]{0:T(512)S(1)} %psum.37), channel_id=1, replica_groups=mesh['blk_0'=2,'blk_1'=4,'blk_2'=4,'blk_3'=2,'grp'=2] {'blk_3'}, use_global_device_ids=true, to_apply=%region_4.0 | all-reduce | flops 512 | bytes 4096 | tf_op jit(solution)/shard_map/psum | solution.py:14
  37.4 5.9 %psum.39 = f32[512]{0:T(512)S(1)} all-reduce(f32[512]{0:T(512)S(1)} %psum.38), channel_id=1, replica_groups=mesh['blk_0'=2,'blk_1'=4,'blk_2'=4,'blk_3'=2,'grp'=2] {'grp'}, use_global_device_ids=true, to_apply=%region_5.0 | all-reduce | flops 512 | bytes 4096 | tf_op jit(solution)/shard_map/psum | solution.py:14
  43.3 1.2 subtract_reduce_fusion
  44.5 1.2 multiply_reduce_fusion
  45.7 1.9 multiply_convert_fusion
  47.6 0.0 all-gather.2.cloned.1.call-update
  47.7 354.2 %all-gather.2.cloned.1.call-done = bf16[512,32768]{1,0:T(8,128)(2,1)} async-done(((bf16[512,256]{1,0:T(8,128)(2,1)}), bf16[512,32768]{1,0:T(8,128)(2,1)}) %all-gather.2.cloned.1.call-update) | async-done | bytes 33554448 | tf_op jit(solution)/shard_map/all_gather | solution.py:37
  401.9 21.2 %fusion = bf16[256,32768]{1,0:T(8,128)(2,1)} fusion(bf16[512,256]{1,0:T(8,128)(2,1)} %multiply_convert_fusion, bf16[512,32768]{1,0:T(8,128)(2,1)} %all-gather.2.cloned.1.call-done, pred[32768]{0:T(1024)(128)(4,1)S(1)} %fusion.1), kind=kOutput, calls=%fused_computation.1 | convolution fusion | flops 8606711808 | bytes 50626560 | tf_op jit(solution)/shard_map/dot_general | solution.py:19
  (4 shorter events, 0.1 us)
Async XLA Ops:
  6.5 395.3 %all-gather.2.cloned.1.call-start = ((), (), s32[]{:S(2)}) async-start(), calls=%async_computation | async-start | bytes 33816576 | tf_op jit(solution)/shard_map/all_gather | solution.py:37
Sparse Core Ops, SparseCore 0:
  47.8 354.0 all-gather.1
where the time goes:
time: 430 us
  waiting for transfers between devices  354 us (82%)
  blocking collectives  35.6 us (8%)
  matrix products  21.2 us (5%)
  between operations  13.4 us (3%)
  other arithmetic  5.51 us (1%)
    all_gather x1, waiting for transfers between devices, shards(): piece = lax.all_gather(zscores, BLK_GRP, axis=1, tiled=True)  354 us
    psum x5, blocking collectives, by_axis(): array = lax.psum(array, axis)  35.6 us
    dot_general x1, matrix products, gram_tile(): lax.dot_general(first, second, (((0,), (0,)), ((), ())), preferred_elemen...  21.2 us
  transfers between devices with their start and end apart: 1, of which 1 were waited for; matrix products, arithmetic and copies ran while one was open for 0% of the time, Pallas kernels for 0%

commit v1 on v0

v1 whole, which is shorter than its diff:
```python
import functools
import math

import jax
import jax.numpy as jnp
from jax import lax
from jax.experimental import pallas as pl
from jax.experimental.pallas import tpu as pltpu
from jax.sharding import PartitionSpec as P

MESH = pl.DeviceIdType.MESH
BARS = 512
SER = 256
HALF = SER // 2

TREE = [
    [(0, 1), (0, 1), (0, 1)], [(0, -1), (0, -1), (0, -1)], [(1, 1), (1, -1), (4, -1)],
    [(4, 1), (3, -1), (1, 1)], [(48, 1), (3, 1), (12, -1)], [(16, -1), (4, 1), (16, 1)],
    [(17, 1), (16, -1), (3, -1)], [(32, -1), (16, 1), (8, 1)], [(13, 1), (15, -1), (17, 1)],
    [(8, 1), (19, -1), (20, 1)], [(7, -1), (52, 1), (15, -1)], [(52, -1), (17, -1), (13, -1)],
    [(49, 1), (17, 1), (7, 1)], [(52, 1), (18, -1), (28, 1)], [(24, -1), (35, 1), (61, -1)],
    [(36, 1), (63, -1), (24, 1)], [(24, 1), (18, 1), (31, 1)], [(56, 1), (14, -1), (6, -1)],
    [(61, 1), (39, 1), (18, 1)], [(59, -1), (45, -1), (22, 1)], [(43, -1), (30, -1), (30, 1)],
]
SLOTS = len(TREE)


def build():
    place = {(0, 0, 0, 0): 0, (0, 0, 0, 1): 1}
    table = []
    for slot, row in enumerate(TREE):
        line = [None] * 6
        for axis, (parent, sign) in enumerate(row):
            for half in range(2):
                way = sign if half == 0 else -sign
                at = [parent % 4, parent // 4 % 4, parent // 16]
                if half:
                    at = [(-v) % 4 for v in at]
                to = list(at)
                to[axis] = (to[axis] + way) % 4
                d = 2 * axis + (way < 0)
                line[d] = (place[(*at, half)], tuple(to), half)
                place[(*to, half)] = 2 + 6 * slot + d
        table.append(line)
    return table


TABLE = build()


def kernel(
    r_ref, out_ref, zbuf, lhs, stage, rt, mtx, mrx,
    mtx_sem, mrx_sem, ltx_sem, lrx_sem, ztx_sem, zrx_sem, ttx_sem, trx_sem,
):
    blk = lax.axis_index("blk")
    grp = lax.axis_index("grp")
    core = blk % 2
    here = [blk // 8 % 4, blk // 2 % 4, grp * 2 + blk // 32]

    def device(at, c):
        x, y, z = at
        return (((z % 2) * 4 + x) * 4 + y) * 2 + c, z // 2

    def block(at, c):
        b, g = device(at, c)
        return b * 2 + g

    def along(axis, step):
        at = list(here)
        at[axis] = (at[axis] + step) % 4
        return device(at, core)

    mine = block(here, core)
    theirs = block(here, 1 - core)
    partner = device(here, 1 - core)
    ring = [[along(axis, step) for step in (1, 2, 3)] for axis in range(3)]

    def send(src, dst, send_sem, recv_sem, to):
        pltpu.make_async_remote_copy(
            src_ref=src, dst_ref=dst, send_sem=send_sem, recv_sem=recv_sem,
            device_id=to, device_id_type=MESH,
        ).start()

    def drain(ref, sem):
        pltpu.make_async_copy(ref, ref, sem).wait()

    barrier = pltpu.get_barrier_semaphore()
    peers = [partner] + [p for line in ring for p in line]
    for p in peers:
        pl.semaphore_signal(barrier, inc=1, device_id=p, device_id_type=MESH)

    turned = r_ref[...].T
    rt[...] = turned
    total = jnp.sum(turned, axis=0, keepdims=True)
    mtx[0] = total
    pl.semaphore_wait(barrier, len(peers))

    send(mtx.at[0], mrx.at[0], mtx_sem.at[0], mrx_sem.at[0], partner)
    drain(mrx.at[0], mrx_sem.at[0])
    total = total + mrx[0]
    for axis in range(3):
        mtx[axis + 1] = total
        for step in range(3):
            send(
                mtx.at[axis + 1], mrx.at[1 + 3 * axis + step],
                mtx_sem.at[axis + 1], mrx_sem.at[axis + 1], ring[axis][step],
            )
        drain(mrx.at[pl.ds(1 + 3 * axis, 3)], mrx_sem.at[axis + 1])
        total = total + (mrx[1 + 3 * axis] + mrx[2 + 3 * axis] + mrx[3 + 3 * axis])
    market = total / (SER * 128)

    excess = rt[...] - market
    deviation = excess - jnp.sum(excess, axis=1, keepdims=True) / BARS
    inverse = lax.rsqrt(
        jnp.sum(deviation * deviation, axis=1, keepdims=True) / BARS + 1e-6
    ) / math.sqrt(BARS)
    z = (deviation * inverse).astype(jnp.bfloat16)
    zbuf[0] = z[:HALF]
    zbuf[1] = z[HALF:]
    lhs[:SER] = z

    next_to = [along(d // 2, -1 if d % 2 else 1) for d in range(6)]

    def forward(slot):
        for d in range(6):
            piece, _, _ = TABLE[slot][d]
            send(
                zbuf.at[piece], zbuf.at[2 + 6 * slot + d],
                ztx_sem.at[slot], zrx_sem.at[slot], next_to[d],
            )

    forward(0)
    send(lhs.at[pl.ds(0, SER)], lhs.at[pl.ds(SER, SER)], ltx_sem, lrx_sem, partner)
    forward(1)

    def tiles(piece, source, half, where, send_sem, recv_sem):
        both = lax.dot_general(
            lhs[...], zbuf[piece], (((1,), (1,)), ((), ())),
            preferred_element_type=jnp.float32,
        )
        column = pl.ds(pl.multiple_of(source * SER + half * HALF, HALF), HALF)
        out_ref[:, column] = jnp.where(source >= mine, both[:SER], 0.0).astype(jnp.bfloat16)
        where[...] = jnp.where(source >= theirs, both[SER:], 0.0).astype(jnp.bfloat16)
        send(where, out_ref.at[:, column], send_sem, recv_sem, partner)

    drain(lhs.at[pl.ds(SER, SER)], lrx_sem)
    for half in range(2):
        tiles(half, mine, half, stage.at[2, half], ttx_sem.at[2], trx_sem.at[SLOTS])

    for slot in range(SLOTS):
        drain(zbuf.at[pl.ds(2 + 6 * slot, 6)], zrx_sem.at[slot])
        if slot + 2 < SLOTS:
            forward(slot + 2)
        bank = slot % 2
        if slot >= 2:
            drain(stage.at[bank], ttx_sem.at[bank])
        codes = [o[0] + 4 * o[1] + 16 * o[2] + 64 * h for _, o, h in TABLE[slot]]

        def one(d, carry, slot=slot, bank=bank, codes=codes):
            code = jnp.int32(codes[0])
            for other in range(1, 6):
                code = jnp.where(d == other, codes[other], code)
            offset = (code % 4, code // 4 % 4, code // 16 % 4)
            source = block([(here[a] + 4 - offset[a]) % 4 for a in range(3)], core)
            tiles(
                2 + 6 * slot + d, source, code // 64, stage.at[bank, d],
                ttx_sem.at[bank], trx_sem.at[slot],
            )
            return carry

        lax.fori_loop(0, 6, one, 0)

    for slot in range(SLOTS):
        drain(zbuf.at[pl.ds(2 + 6 * slot, 6)], ztx_sem.at[slot])
        drain(stage.at[0], trx_sem.at[slot])
    drain(stage.at[0], ttx_sem.at[0])
    drain(stage.at[1], ttx_sem.at[1])
    drain(stage.at[2, pl.ds(0, 2)], ttx_sem.at[2])
    drain(stage.at[2, pl.ds(0, 2)], trx_sem.at[SLOTS])
    drain(lhs.at[pl.ds(0, SER)], ltx_sem)
    drain(mtx.at[0], mtx_sem.at[0])
    for axis in range(3):
        drain(mrx.at[pl.ds(1 + 3 * axis, 3)], mtx_sem.at[axis + 1])


def shards(returns):
    dma = pltpu.SemaphoreType.DMA
    return pl.pallas_call(
        kernel,
        out_shape=pltpu.VMEM((SER, 128 * SER), jnp.bfloat16),
        in_specs=[pl.BlockSpec(memory_space=pltpu.VMEM)],
        out_specs=pl.BlockSpec(memory_space=pltpu.VMEM),
        scratch_shapes=[
            pltpu.VMEM((128, HALF, BARS), jnp.bfloat16),
            pltpu.VMEM((2 * SER, BARS), jnp.bfloat16),
            pltpu.VMEM((3, 6, SER, HALF), jnp.bfloat16),
            pltpu.VMEM((SER, BARS), jnp.float32),
            pltpu.VMEM((4, 1, BARS), jnp.float32),
            pltpu.VMEM((10, 1, BARS), jnp.float32),
            dma((4,)), dma((4,)), dma, dma,
            dma((SLOTS,)), dma((SLOTS,)), dma((3,)), dma((SLOTS + 1,)),
        ],
        compiler_params=pltpu.CompilerParams(
            collective_id=0, has_side_effects=True, vmem_limit_bytes=30 * 2**20
        ),
    )(returns)


def solution(mesh):
    axes = ("blk", "grp")
    return jax.shard_map(
        shards, mesh=mesh, in_specs=(P(None, axes),), out_specs=P(axes, None), check_vma=False
    )
```

time: 430 us -> 89.9 us (0.21)
  waiting for transfers between devices: 354 us -> 0 us
  Pallas kernels: 0 us -> 82.6 us
  blocking collectives: 35.6 us -> 0 us
  matrix products: 21.2 us -> 0 us
  between operations: 13.4 us -> 0.01 us
  local copies, waits for them, and re-layouts: 0 us -> 7.2 us
  other arithmetic: 5.51 us -> 0 us
    all_gather x1 -> x0, waiting for transfers between devices: 354 us -> none  [shards(): piece = lax.all_gather(zscores, BLK_GRP, axis=1, tiled=True)]
    pallas_call x0 -> x1, Pallas kernels: none -> 82.6 us  [shards(): pl.pallas_call(kernel, out_shape=pltpu.VMEM((SER, 128 * SER), jnp.bfloat1...]
    psum x5 -> x0, blocking collectives: 35.6 us -> none  [by_axis(): array = lax.psum(array, axis)]
    dot_general x1 -> x0, matrix products: 21.2 us -> none  [gram_tile(): lax.dot_general(first, second, (((0,), (0,)), ((), ())), preferred_elemen...]
    unnamed x0 -> x3, local copies, waits for them, and re-layouts: none -> 7.2 us
  transfers between devices with their start and end apart: 1 -> 0, of which waited for: 1 -> 0; matrix products, arithmetic and copies ran while one was open for 0% -> 0% of each run, Pallas kernels for 0% -> 0%
where the time goes in v1:
time: 89.9 us; the launch traced here: 89.8 us
  Pallas kernels  82.6 us (92%)
  local copies, waits for them, and re-layouts  7.2 us (8%)
    pallas_call x1, Pallas kernels, shards(): pl.pallas_call(kernel, out_shape=pltpu.VMEM((SER, 128 * SER), jnp.bfloat1...  82.6 us
    unnamed x3, local copies, waits for them, and re-layouts  7.2 us

profile of v1, /device:TPU:1, one launch (start us, length us, event | category | flops | bytes accessed | tf_op | source)
XLA Modules:
  0.0 89.8 jit_solution(17904464689091142038)
XLA Ops:
  0.0 0.0 copy-start
  0.0 1.0 %copy-done = f32[512,256]{1,0:T(8,128)S(1)} copy-done((f32[512,256]{1,0:T(8,128)S(1)}, f32[512,256]{1,0:T(8,128)}, u32[]{:S(2)}) %copy-start) | copy-done | bytes 524312
  1.0 82.6 %shard_map.17 = bf16[256,32768]{1,0:T(8,128)(2,1)S(1)} custom-call(f32[512,256]{1,0:T(8,128)S(1)} %copy-done), custom_call_target="tpu_custom_call" | custom-call | tf_op jit(solution)/shard_map/pallas_call | solution.py:188
  83.6 6.2 %copy.3 = bf16[256,32768]{1,0:T(8,128)(2,1)} copy(bf16[256,32768]{1,0:T(8,128)(2,1)S(1)} %shard_map.17) | data formatting | bytes 33554432
Async XLA Ops:
  0.0 1.0 %copy-start = (f32[512,256]{1,0:T(8,128)S(1)}, f32[512,256]{1,0:T(8,128)}, u32[]{:S(2)}) copy-start(f32[512,256]{1,0:T(8,128)} %r_ref.1) | copy-start | bytes 1572868

commit v2 on v1

--- a/solution.py
+++ b/solution.py
@@ -12,6 +12,7 @@
 BARS = 512
 SER = 256
 HALF = SER // 2
+PARTS = 8
 
 TREE = [
     [(0, 1), (0, 1), (0, 1)], [(0, -1), (0, -1), (0, -1)], [(1, 1), (1, -1), (4, -1)],
@@ -49,9 +50,11 @@
 
 
 def kernel(
-    r_ref, out_ref, zbuf, lhs, stage, rt, mtx, mrx,
-    mtx_sem, mrx_sem, ltx_sem, lrx_sem, ztx_sem, zrx_sem, ttx_sem, trx_sem,
+    r_ref, out_ref, zbuf, lhs, stage, inp, rt, raw, mrx,
+    in_sem, mtx_sem, mrx_sem, wtx_sem, wrx_sem, ltx_sem, lrx_sem, ztx_sem, zrx_sem, ttx_sem, trx_sem,
 ):
+    load = pltpu.make_async_copy(r_ref, inp, in_sem)
+    load.start()
     blk = lax.axis_index("blk")
     grp = lax.axis_index("grp")
     core = blk % 2
@@ -65,15 +68,15 @@
         b, g = device(at, c)
         return b * 2 + g
 
-    def along(axis, step):
+    def along(axis, step, c):
         at = list(here)
         at[axis] = (at[axis] + step) % 4
-        return device(at, core)
+        return device(at, c)
 
     mine = block(here, core)
     theirs = block(here, 1 - core)
     partner = device(here, 1 - core)
-    ring = [[along(axis, step) for step in (1, 2, 3)] for axis in range(3)]
+    next_to = [along(d // 2, -1 if d % 2 else 1, core) for d in range(6)]
 
     def send(src, dst, send_sem, recv_sem, to):
         pltpu.make_async_remote_copy(
@@ -85,53 +88,99 @@
         pltpu.make_async_copy(ref, ref, sem).wait()
 
     barrier = pltpu.get_barrier_semaphore()
-    peers = [partner] + [p for line in ring for p in line]
+    peers = [partner]
+    for axis in range(3):
+        for step in (2, 1, 3):
+            peers.append(along(axis, step, core))
+            if axis != 1:
+                peers.append(along(axis, step, 1 - core))
     for p in peers:
         pl.semaphore_signal(barrier, inc=1, device_id=p, device_id_type=MESH)
 
-    turned = r_ref[...].T
+    load.wait()
+    turned = inp[...].T
     rt[...] = turned
-    total = jnp.sum(turned, axis=0, keepdims=True)
-    mtx[0] = total
+    first = here[0] * 2 + core
+    mrx[first] = jnp.sum(turned, axis=0, keepdims=True)
     pl.semaphore_wait(barrier, len(peers))
 
-    send(mtx.at[0], mrx.at[0], mtx_sem.at[0], mrx_sem.at[0], partner)
-    drain(mrx.at[0], mrx_sem.at[0])
-    total = total + mrx[0]
-    for axis in range(3):
-        mtx[axis + 1] = total
-        for step in range(3):
-            send(
-                mtx.at[axis + 1], mrx.at[1 + 3 * axis + step],
-                mtx_sem.at[axis + 1], mrx_sem.at[axis + 1], ring[axis][step],
-            )
-        drain(mrx.at[pl.ds(1 + 3 * axis, 3)], mrx_sem.at[axis + 1])
-        total = total + (mrx[1 + 3 * axis] + mrx[2 + 3 * axis] + mrx[3 + 3 * axis])
-    market = total / (SER * 128)
-
-    excess = rt[...] - market
-    deviation = excess - jnp.sum(excess, axis=1, keepdims=True) / BARS
-    inverse = lax.rsqrt(
-        jnp.sum(deviation * deviation, axis=1, keepdims=True) / BARS + 1e-6
-    ) / math.sqrt(BARS)
-    z = (deviation * inverse).astype(jnp.bfloat16)
-    zbuf[0] = z[:HALF]
-    zbuf[1] = z[HALF:]
-    lhs[:SER] = z
-
-    next_to = [along(d // 2, -1 if d % 2 else 1) for d in range(6)]
-
-    def forward(slot):
+    def bulk(d):
+        send(rt.at[pl.ds((d % 2) * HALF, HALF)], raw.at[d], wtx_sem, wrx_sem, next_to[d])
+
+    def ring_sum(low, count):
+        total = mrx[low]
+        for n in range(1, count):
+            total = total + mrx[low + n]
+        return total
+
+    def sum_to(slot, low, axis, c, phase):
+        for step in (2, 1, 3):
+            send(mrx.at[slot], mrx.at[slot], mtx_sem.at[phase], mrx_sem.at[phase], along(axis, step, c))
+
+    @pl.when(core == 0)
+    def _():
+        send(mrx.at[first], mrx.at[first], mtx_sem.at[0], mrx_sem.at[0], partner)
+        sum_to(first, 0, 0, 1, 0)
         for d in range(6):
-            piece, _, _ = TABLE[slot][d]
-            send(
-                zbuf.at[piece], zbuf.at[2 + 6 * slot + d],
-                ztx_sem.at[slot], zrx_sem.at[slot], next_to[d],
-            )
-
-    forward(0)
+            bulk(d)
+        drain(mrx.at[pl.ds(12, 4)], mrx_sem.at[2])
+        drain(mrx.at[pl.ds(0, 4)], mtx_sem.at[0])
+
+    @pl.when(core == 1)
+    def _():
+        sum_to(first, 0, 0, 1, 0)
+        for d in (0, 1, 4, 5):
+            bulk(d)
+        drain(mrx.at[pl.ds(0, 7)], mrx_sem.at[0])
+        second = 8 + here[1]
+        mrx[second] = ring_sum(0, 8)
+        sum_to(second, 8, 1, 1, 1)
+        bulk(2)
+        bulk(3)
+        drain(mrx.at[pl.ds(8, 3)], mrx_sem.at[1])
+        third = 12 + here[2]
+        mrx[third] = ring_sum(8, 4)
+        sum_to(third, 12, 2, 1, 2)
+        sum_to(third, 12, 2, 0, 2)
+        send(mrx.at[third], mrx.at[third], mtx_sem.at[2], mrx_sem.at[2], partner)
+        drain(mrx.at[pl.ds(12, 3)], mrx_sem.at[2])
+        drain(mrx.at[pl.ds(0, 3)], mtx_sem.at[0])
+        drain(mrx.at[pl.ds(8, 3)], mtx_sem.at[1])
+        drain(mrx.at[pl.ds(0, 7)], mtx_sem.at[2])
+
+    market = ring_sum(12, 4) / (SER * 128)
+
+    def zscore(series):
+        excess = series - market
+        deviation = excess - jnp.sum(excess, axis=1, keepdims=True) / BARS
+        inverse = lax.rsqrt(
+            jnp.sum(deviation * deviation, axis=1, keepdims=True) / BARS + 1e-6
+        ) / math.sqrt(BARS)
+        return (deviation * inverse).astype(jnp.bfloat16)
+
+    def forward(slot, d):
+        send(
+            zbuf.at[TABLE[slot][d][0]], zbuf.at[2 + 6 * slot + d],
+            ztx_sem.at[slot], zrx_sem.at[slot], next_to[d],
+        )
+
+    for half in range(2):
+        z = zscore(rt[half * HALF:(half + 1) * HALF])
+        zbuf[half] = z
+        lhs[half * HALF:(half + 1) * HALF] = z
+        for d in range(6):
+            if TABLE[1][d][0] == half:
+                forward(1, d)
     send(lhs.at[pl.ds(0, SER)], lhs.at[pl.ds(SER, SER)], ltx_sem, lrx_sem, partner)
-    forward(1)
+    drain(raw, wrx_sem)
+
+    def from_raw(d, carry):
+        zbuf[2 + d] = zscore(raw[d])
+        return carry
+
+    lax.fori_loop(0, 6, from_raw, 0)
+    for d in range(6):
+        forward(2, d)
 
     def tiles(piece, source, half, where, send_sem, recv_sem):
         both = lax.dot_general(
@@ -148,9 +197,10 @@
         tiles(half, mine, half, stage.at[2, half], ttx_sem.at[2], trx_sem.at[SLOTS])
 
     for slot in range(SLOTS):
-        drain(zbuf.at[pl.ds(2 + 6 * slot, 6)], zrx_sem.at[slot])
-        if slot + 2 < SLOTS:
-            forward(slot + 2)
+        if slot:
+            drain(zbuf.at[pl.ds(2 + 6 * slot, 6)], zrx_sem.at[slot])
+            for d in range(6 if slot + 2 < SLOTS else 0):
+                forward(slot + 2, d)
         bank = slot % 2
         if slot >= 2:
             drain(stage.at[bank], ttx_sem.at[bank])
@@ -171,39 +221,58 @@
         lax.fori_loop(0, 6, one, 0)
 
     for slot in range(SLOTS):
-        drain(zbuf.at[pl.ds(2 + 6 * slot, 6)], ztx_sem.at[slot])
+        if slot:
+            drain(zbuf.at[pl.ds(2 + 6 * slot, 6)], ztx_sem.at[slot])
         drain(stage.at[0], trx_sem.at[slot])
     drain(stage.at[0], ttx_sem.at[0])
     drain(stage.at[1], ttx_sem.at[1])
     drain(stage.at[2, pl.ds(0, 2)], ttx_sem.at[2])
     drain(stage.at[2, pl.ds(0, 2)], trx_sem.at[SLOTS])
     drain(lhs.at[pl.ds(0, SER)], ltx_sem)
-    drain(mtx.at[0], mtx_sem.at[0])
-    for axis in range(3):
-        drain(mrx.at[pl.ds(1 + 3 * axis, 3)], mtx_sem.at[axis + 1])
+    drain(raw, wtx_sem)
+
+
+def write_out(held_ref, out_ref, sem):
+    rows = SER // PARTS
+    copies = []
+    for n in range(PARTS):
+        part = pl.ds(n * rows, rows)
+        copies.append(pltpu.make_async_copy(held_ref.at[part], out_ref.at[part], sem.at[n]))
+        copies[n].start()
+    for copy in copies:
+        copy.wait()
 
 
 def shards(returns):
     dma = pltpu.SemaphoreType.DMA
-    return pl.pallas_call(
+    held = pl.pallas_call(
         kernel,
         out_shape=pltpu.VMEM((SER, 128 * SER), jnp.bfloat16),
-        in_specs=[pl.BlockSpec(memory_space=pltpu.VMEM)],
+        in_specs=[pl.BlockSpec(memory_space=pltpu.HBM)],
         out_specs=pl.BlockSpec(memory_space=pltpu.VMEM),
         scratch_shapes=[
             pltpu.VMEM((128, HALF, BARS), jnp.bfloat16),
             pltpu.VMEM((2 * SER, BARS), jnp.bfloat16),
             pltpu.VMEM((3, 6, SER, HALF), jnp.bfloat16),
+            pltpu.VMEM((BARS, SER), jnp.float32),
             pltpu.VMEM((SER, BARS), jnp.float32),
-            pltpu.VMEM((4, 1, BARS), jnp.float32),
-            pltpu.VMEM((10, 1, BARS), jnp.float32),
-            dma((4,)), dma((4,)), dma, dma,
+            pltpu.VMEM((6, HALF, BARS), jnp.float32),
+            pltpu.VMEM((16, 1, BARS), jnp.float32),
+            dma, dma((3,)), dma((3,)), dma, dma, dma, dma,
             dma((SLOTS,)), dma((SLOTS,)), dma((3,)), dma((SLOTS + 1,)),
         ],
         compiler_params=pltpu.CompilerParams(
             collective_id=0, has_side_effects=True, vmem_limit_bytes=30 * 2**20
         ),
-    )(returns)
+    )(pltpu.with_memory_space_constraint(returns, pltpu.HBM))
+    return pl.pallas_call(
+        write_out,
+        out_shape=jax.ShapeDtypeStruct((SER, 128 * SER), jnp.bfloat16),
+        in_specs=[pl.BlockSpec(memory_space=pltpu.VMEM)],
+        out_specs=pl.BlockSpec(memory_space=pl.ANY),
+        scratch_shapes=[dma((PARTS,))],
+        compiler_params=pltpu.CompilerParams(vmem_limit_bytes=2**20),
+    )(pltpu.with_memory_space_constraint(held, pltpu.VMEM))
 
 
 def solution(mesh):

time: 89.9 us -> 86.6 us (0.963)
  local copies, waits for them, and re-layouts: 7.2 us -> 0 us
  Pallas kernels: 82.6 us -> 86.5 us
    unnamed x3 -> x0, local copies, waits for them, and re-layouts: 7.2 us -> none
    pallas_call x0 -> x1, Pallas kernels: none -> 5.92 us  [shards(): pl.pallas_call(write_out, out_shape=jax.ShapeDtypeStruct((SER, 128 * SER)...]
    pallas_call x1, Pallas kernels: 82.6 us -> 80.6 us  [shards(): pl.pallas_call(kernel, out_shape=pltpu.VMEM((SER, 128 * SER), jnp.bfloat1...]
where the time goes in v2:
time: 86.6 us; the launch traced here: 86.5 us
  Pallas kernels  86.5 us (100%)
    pallas_call x1, Pallas kernels, shards(): pl.pallas_call(kernel, out_shape=pltpu.VMEM((SER, 128 * SER), jnp.bfloat1...  80.6 us
    pallas_call x1, Pallas kernels, shards(): pl.pallas_call(write_out, out_shape=jax.ShapeDtypeStruct((SER, 128 * SER)...  5.92 us

profile of v2, /device:TPU:1, one launch (start us, length us, event | category | flops | bytes accessed | tf_op | source)
XLA Modules:
  0.0 86.5 jit_solution(161132937925806621)
XLA Ops:
  0.0 80.6 %shard_map.17.held_ref = bf16[256,32768]{1,0:T(8,128)(2,1)S(1)} custom-call(f32[512,256]{1,0:T(8,128)} %r_ref.1), custom_call_target="tpu_custom_call" | custom-call | tf_op jit(solution)/shard_map/pallas_call | solution.py:248
  80.6 5.9 %shard_map.18 = bf16[256,32768]{1,0:T(8,128)(2,1)} custom-call(bf16[256,32768]{1,0:T(8,128)(2,1)S(1)} %shard_map.17.held_ref), custom_call_target="tpu_custom_call" | custom-call | tf_op jit(solution)/shard_map/pallas_call | solution.py:268

commit v3 on v2

v3 whole, which is shorter than its diff:
```python
import functools
import math

import jax
import jax.numpy as jnp
from jax import lax
from jax.experimental import pallas as pl
from jax.experimental.pallas import tpu as pltpu
from jax.sharding import PartitionSpec as P

MESH = pl.DeviceIdType.MESH
BARS = 512
SER = 256
HALF = SER // 2
PARTS = 8
DEPTH = 4
QUARTER = HALF // 2
CHUNKS = 4

TREE = [
    [(0, 1), (0, 1), (0, 1)], [(0, -1), (0, -1), (0, -1)], [(1, 1), (1, -1), (4, -1)],
    [(4, 1), (3, -1), (1, 1)], [(48, 1), (3, 1), (12, -1)], [(16, -1), (4, 1), (16, 1)],
    [(17, 1), (16, -1), (3, -1)], [(32, -1), (16, 1), (8, 1)], [(13, 1), (15, -1), (17, 1)],
    [(8, 1), (19, -1), (20, 1)], [(7, -1), (52, 1), (15, -1)], [(52, -1), (17, -1), (13, -1)],
    [(49, 1), (17, 1), (7, 1)], [(52, 1), (18, -1), (28, 1)], [(24, -1), (35, 1), (61, -1)],
    [(36, 1), (63, -1), (24, 1)], [(24, 1), (18, 1), (31, 1)], [(56, 1), (14, -1), (6, -1)],
    [(61, 1), (39, 1), (18, 1)], [(59, -1), (45, -1), (22, 1)], [(43, -1), (30, -1), (30, 1)],
]
SLOTS = len(TREE)


def build():
    place = {(0, 0, 0, 0): 0, (0, 0, 0, 1): 1}
    table = []
    for slot, row in enumerate(TREE):
        line = [None] * 6
        for axis, (parent, sign) in enumerate(row):
            for half in range(2):
                way = sign if half == 0 else -sign
                at = [parent % 4, parent // 4 % 4, parent // 16]
                if half:
                    at = [(-v) % 4 for v in at]
                to = list(at)
                to[axis] = (to[axis] + way) % 4
                d = 2 * axis + (way < 0)
                line[d] = (place[(*at, half)], tuple(to), half)
                place[(*to, half)] = 2 + 6 * slot + d
        table.append(line)
    return table


TABLE = build()


def issue_plan():
    plan = [[] for _ in range(SLOTS)]
    when = [0] * 6
    for slot in range(2, SLOTS):
        for d in range(6):
            when[d] = max((TABLE[slot][d][0] - 2) // 6, when[d], slot - DEPTH)
            plan[when[d]].append((slot, d))
    return plan


PLAN = issue_plan()


def kernel(
    r_ref, out_ref, zbuf, lhs, stage, inp, rt, raw, early, mrx,
    in_sem, mtx_sem, mrx_sem, wtx_sem, wrx_sem, ltx_sem, lrx_sem, ztx_sem, zrx_sem, ttx_sem, trx_sem,
):
    span = BARS // CHUNKS
    loads = []
    for q in range(CHUNKS):
        part = pl.ds(q * span, span)
        loads.append(pltpu.make_async_copy(r_ref.at[part], inp.at[part], in_sem.at[q]))
        loads[q].start()
    blk = lax.axis_index("blk")
    grp = lax.axis_index("grp")
    core = blk % 2
    here = [blk // 8 % 4, blk // 2 % 4, grp * 2 + blk // 32]

    def device(at, c):
        x, y, z = at
        return (((z % 2) * 4 + x) * 4 + y) * 2 + c, z // 2

    def block(at, c):
        b, g = device(at, c)
        return b * 2 + g

    def away(x, y, z, c):
        return device([(here[0] + x) % 4, (here[1] + y) % 4, (here[2] + z) % 4], c)

    mine = block(here, core)
    theirs = block(here, 1 - core)
    partner = device(here, 1 - core)
    steps = [(1, 0, 0), (3, 0, 0), (0, 1, 0), (0, 3, 0), (0, 0, 1), (0, 0, 3)]
    next_to = [away(*step, core) for step in steps]
    ring = [(x, 0, 0) for x in (2, 1, 3)]
    plane = [(0, y, z) for y in (2, 1, 3, 0) for z in (2, 1, 3, 0) if (y, z) != (0, 0)]

    def send(src, dst, send_sem, recv_sem, to):
        pltpu.make_async_remote_copy(
            src_ref=src, dst_ref=dst, send_sem=send_sem, recv_sem=recv_sem,
            device_id=to, device_id_type=MESH,
        ).start()

    def drain(ref, sem):
        pltpu.make_async_copy(ref, ref, sem).wait()

    barrier = pltpu.get_barrier_semaphore()

    def greet(devices):
        for to in devices:
            pl.semaphore_signal(barrier, inc=1, device_id=to, device_id_type=MESH)
        return len(devices)

    zero_peers = [partner] + [away(*o, 1 - core) for o in ring] + next_to
    one_peers = zero_peers[:4] + [away(*o, core) for o in plane + ring]

    @pl.when(core == 0)
    def _():
        greet(zero_peers)

    @pl.when(core == 1)
    def _():
        greet(one_peers)

    first = here[0] * 2 + core
    for q in range(CHUNKS):
        loads[q].wait()
        bars = inp[q * span:(q + 1) * span]
        pairs = bars[:, :HALF] + bars[:, HALF:]
        mrx[first, :, q * span:(q + 1) * span] = jnp.sum(pairs.T, axis=0, keepdims=True)

    def add_up(low, count):
        total = mrx[low]
        for n in range(1, count):
            total = total + mrx[low + n]
        return total

    def raw_first(d):
        send(rt.at[pl.ds((d % 2) * HALF, HALF)], raw.at[d], wtx_sem.at[0], wrx_sem.at[0], next_to[d])

    def raw_second(d):
        rows = pl.ds((1 - d % 2) * HALF, QUARTER)
        send(rt.at[rows], early.at[d], wtx_sem.at[1], wrx_sem.at[1], next_to[d])

    def turn():
        for q in range(CHUNKS):
            rt[:, q * span:(q + 1) * span] = inp[q * span:(q + 1) * span].T

    @pl.when(core == 0)
    def _():
        pl.semaphore_wait(barrier, len(zero_peers))
        send(mrx.at[first], mrx.at[first], mtx_sem.at[0], mrx_sem.at[0], partner)
        for o in ring:
            send(mrx.at[first], mrx.at[first], mtx_sem.at[0], mrx_sem.at[0], away(*o, 1))
        turn()
        for d in range(6):
            raw_first(d)
        for d in range(6):
            raw_second(d)
        drain(mrx.at[24], mrx_sem.at[2])
        drain(mrx.at[pl.ds(0, 4)], mtx_sem.at[0])

    @pl.when(core == 1)
    def _():
        pl.semaphore_wait(barrier, len(one_peers))
        for o in ring:
            send(mrx.at[first], mrx.at[first], mtx_sem.at[0], mrx_sem.at[0], away(*o, 1))
        turn()
        for d in (2, 3, 4, 5):
            raw_second(d)
        for d in (0, 1):
            raw_first(d)
            raw_second(d)
        drain(mrx.at[pl.ds(0, 7)], mrx_sem.at[0])
        second = 8 + here[1] * 4 + here[2]
        mrx[second] = add_up(0, 8)
        for o in plane:
            send(mrx.at[second], mrx.at[second], mtx_sem.at[1], mrx_sem.at[1], away(*o, 1))
        for d in (2, 3, 4, 5):
            raw_first(d)
        drain(mrx.at[pl.ds(8, 15)], mrx_sem.at[1])
        mrx[24] = add_up(8, 16)
        send(mrx.at[24], mrx.at[24], mtx_sem.at[2], mrx_sem.at[2], partner)
        drain(mrx.at[pl.ds(0, 3)], mtx_sem.at[0])
        drain(mrx.at[pl.ds(8, 15)], mtx_sem.at[1])
        drain(mrx.at[24], mtx_sem.at[2])

    market = mrx[24] / (SER * 128)

    def zscore(series):
        excess = series - market
        deviation = excess - jnp.sum(excess, axis=1, keepdims=True) / BARS
        inverse = lax.rsqrt(
            jnp.sum(deviation * deviation, axis=1, keepdims=True) / BARS + 1e-6
        ) / math.sqrt(BARS)
        return (deviation * inverse).astype(jnp.bfloat16)

    def forward(slot, d):
        send(
            zbuf.at[TABLE[slot][d][0]], zbuf.at[2 + 6 * slot + d],
            ztx_sem.at[slot], zrx_sem.at[slot], next_to[d],
        )

    late = pl.ds(QUARTER, QUARTER)
    for half in range(2):
        z = zscore(rt[half * HALF:(half + 1) * HALF])
        zbuf[half] = z
        lhs[half * HALF:(half + 1) * HALF] = z
        for d in range(6):
            if TABLE[1][d][0] == half:
                send(
                    zbuf.at[half, late], zbuf.at[8 + d, late],
                    ztx_sem.at[1], zrx_sem.at[1], next_to[d],
                )
    send(lhs.at[pl.ds(0, SER)], lhs.at[pl.ds(SER, SER)], ltx_sem, lrx_sem, partner)

    drain(raw, wrx_sem.at[0])
    waiting = list(PLAN[0])
    for n in range(6):
        zbuf[2 + n] = zscore(raw[n])
        held = set()
        for slot, d in list(waiting):
            if d in held or TABLE[slot][d][0] > 2 + n:
                held.add(d)
            else:
                forward(slot, d)
                waiting.remove((slot, d))
    drain(early, wrx_sem.at[1])

    def from_early(d, carry):
        zbuf[8 + d, :QUARTER] = zscore(early[d])
        return carry

    lax.fori_loop(0, 6, from_early, 0)

    def tiles(piece, sources, halves, where, send_sem, recv_sem):
        both = lax.dot_general(
            lhs[...], zbuf[pl.ds(piece, 2)].reshape(SER, BARS), (((1,), (1,)), ((), ())),
            preferred_element_type=jnp.float32,
        )
        for n in range(2):
            part = both[:, n * HALF:(n + 1) * HALF]
            column = pl.ds(pl.multiple_of(sources[n] * SER + halves[n] * HALF, HALF), HALF)
            where[n] = jnp.where(sources[n] >= theirs, part[SER:], 0.0).astype(jnp.bfloat16)
            out_ref[:, column] = jnp.where(sources[n] >= mine, part[:SER], 0.0).astype(jnp.bfloat16)
            send(where.at[n], out_ref.at[:, column], send_sem, recv_sem, partner)

    def landed(slot):
        if slot == 1:
            return zbuf.at[pl.ds(8, 6), late]
        return zbuf.at[pl.ds(2 + 6 * slot, 6)]

    drain(lhs.at[pl.ds(SER, SER)], lrx_sem)
    tiles(
        0, (mine, mine), (0, 1), stage.at[2, pl.ds(0, 2)], ttx_sem.at[2], trx_sem.at[SLOTS]
    )

    for slot in range(SLOTS):
        if slot:
            drain(landed(slot), zrx_sem.at[slot])
            for later, d in PLAN[slot]:
                forward(later, d)
        bank = slot % 2
        if slot >= 2:
            drain(stage.at[bank], ttx_sem.at[bank])
        codes = [o[0] + 4 * o[1] + 16 * o[2] + 64 * h for _, o, h in TABLE[slot]]

        def one(axis, carry, slot=slot, bank=bank, codes=codes):
            sources, halves = [], []
            for n in range(2):
                code = jnp.where(axis == 0, codes[n], jnp.where(axis == 1, codes[2 + n], codes[4 + n]))
                offset = (code % 4, code // 4 % 4, code // 16 % 4)
                sources.append(block([(here[a] + 4 - offset[a]) % 4 for a in range(3)], core))
                halves.append(code // 64)
            tiles(
                2 + 6 * slot + 2 * axis, sources, halves, stage.at[bank, pl.ds(2 * axis, 2)],
                ttx_sem.at[bank], trx_sem.at[slot],
            )
            return carry

        lax.fori_loop(0, 3, one, 0)

    for slot in range(SLOTS):
        if slot:
            drain(landed(slot), ztx_sem.at[slot])
        drain(stage.at[0], trx_sem.at[slot])
    drain(stage.at[0], ttx_sem.at[0])
    drain(stage.at[1], ttx_sem.at[1])
    drain(stage.at[2, pl.ds(0, 2)], ttx_sem.at[2])
    drain(stage.at[2, pl.ds(0, 2)], trx_sem.at[SLOTS])
    drain(lhs.at[pl.ds(0, SER)], ltx_sem)
    drain(raw, wtx_sem.at[0])
    drain(early, wtx_sem.at[1])


def write_out(held_ref, out_ref, sem):
    rows = SER // PARTS
    copies = []
    for n in range(PARTS):
        part = pl.ds(n * rows, rows)
        copies.append(pltpu.make_async_copy(held_ref.at[part], out_ref.at[part], sem.at[n]))
        copies[n].start()
    for copy in copies:
        copy.wait()


def shards(returns):
    dma = pltpu.SemaphoreType.DMA
    held = pl.pallas_call(
        kernel,
        out_shape=pltpu.VMEM((SER, 128 * SER), jnp.bfloat16),
        in_specs=[pl.BlockSpec(memory_space=pltpu.HBM)],
        out_specs=pl.BlockSpec(memory_space=pltpu.VMEM),
        scratch_shapes=[
            pltpu.VMEM((128, HALF, BARS), jnp.bfloat16),
            pltpu.VMEM((2 * SER, BARS), jnp.bfloat16),
            pltpu.VMEM((3, 6, SER, HALF), jnp.bfloat16),
            pltpu.VMEM((BARS, SER), jnp.float32),
            pltpu.VMEM((SER, BARS), jnp.float32),
            pltpu.VMEM((6, HALF, BARS), jnp.float32),
            pltpu.VMEM((6, QUARTER, BARS), jnp.float32),
            pltpu.VMEM((25, 1, BARS), jnp.float32),
            dma((CHUNKS,)), dma((3,)), dma((3,)), dma((2,)), dma((2,)), dma, dma,
            dma((SLOTS,)), dma((SLOTS,)), dma((3,)), dma((SLOTS + 1,)),
        ],
        compiler_params=pltpu.CompilerParams(
            collective_id=0, has_side_effects=True, vmem_limit_bytes=30 * 2**20
        ),
    )(pltpu.with_memory_space_constraint(returns, pltpu.HBM))
    return pl.pallas_call(
        write_out,
        out_shape=jax.ShapeDtypeStruct((SER, 128 * SER), jnp.bfloat16),
        in_specs=[pl.BlockSpec(memory_space=pltpu.VMEM)],
        out_specs=pl.BlockSpec(memory_space=pl.ANY),
        scratch_shapes=[dma((PARTS,))],
        compiler_params=pltpu.CompilerParams(vmem_limit_bytes=2**20),
    )(pltpu.with_memory_space_constraint(held, pltpu.VMEM))


def solution(mesh):
    axes = ("blk", "grp")
    return jax.shard_map(
        shards, mesh=mesh, in_specs=(P(None, axes),), out_specs=P(axes, None), check_vma=False
    )
```

time: 86.6 us -> 84.8 us (0.979)
  Pallas kernels: 86.5 us -> 84.7 us
    pallas_call x1, Pallas kernels: 80.6 us -> 78.8 us  [shards(): pl.pallas_call(kernel, out_shape=pltpu.VMEM((SER, 128 * SER), jnp.bfloat1...]
where the time goes in v3:
time: 84.8 us; the launch traced here: 84.7 us
  Pallas kernels  84.7 us (100%)
    pallas_call x1, Pallas kernels, shards(): pl.pallas_call(kernel, out_shape=pltpu.VMEM((SER, 128 * SER), jnp.bfloat1...  78.8 us
    pallas_call x1, Pallas kernels, shards(): pl.pallas_call(write_out, out_shape=jax.ShapeDtypeStruct((SER, 128 * SER)...  5.92 us

profile of v3, /device:TPU:1, one launch (start us, length us, event | category | flops | bytes accessed | tf_op | source)
XLA Modules:
  0.0 84.7 jit_solution(18375603871583109940)
XLA Ops:
  0.0 78.8 %shard_map.17.held_ref = bf16[256,32768]{1,0:T(8,128)(2,1)S(1)} custom-call(f32[512,256]{1,0:T(8,128)} %r_ref.1), custom_call_target="tpu_custom_call" | custom-call | tf_op jit(solution)/shard_map/pallas_call | solution.py:313
  78.8 5.9 %shard_map.18 = bf16[256,32768]{1,0:T(8,128)(2,1)} custom-call(bf16[256,32768]{1,0:T(8,128)(2,1)S(1)} %shard_map.17.held_ref), custom_call_target="tpu_custom_call" | custom-call | tf_op jit(solution)/shard_map/pallas_call | solution.py:334

commit v4 on v3

--- a/solution.py
+++ b/solution.py
@@ -14,6 +14,7 @@
 HALF = SER // 2
 PARTS = 8
 DEPTH = 4
+BEHIND = 3
 QUARTER = HALF // 2
 CHUNKS = 4
 
@@ -67,7 +68,8 @@
 
 def kernel(
     r_ref, out_ref, zbuf, lhs, stage, inp, rt, raw, early, mrx,
-    in_sem, mtx_sem, mrx_sem, wtx_sem, wrx_sem, ltx_sem, lrx_sem, ztx_sem, zrx_sem, ttx_sem, trx_sem,
+    in_sem, mtx_sem, mrx_sem, wtx_sem, wrx_sem, etx_sem, erx_sem,
+    ltx_sem, lrx_sem, ztx_sem, zrx_sem, ttx_sem, trx_sem,
 ):
     span = BARS // CHUNKS
     loads = []
@@ -115,16 +117,16 @@
             pl.semaphore_signal(barrier, inc=1, device_id=to, device_id_type=MESH)
         return len(devices)
 
-    zero_peers = [partner] + [away(*o, 1 - core) for o in ring] + next_to
-    one_peers = zero_peers[:4] + [away(*o, core) for o in plane + ring]
+    ring_peers = [partner] + [away(*o, 1 - core) for o in ring]
+    one_peers = [away(*o, 1) for o in plane]
 
     @pl.when(core == 0)
     def _():
-        greet(zero_peers)
+        greet(ring_peers + next_to + one_peers)
 
     @pl.when(core == 1)
     def _():
-        greet(one_peers)
+        greet(ring_peers + one_peers + [away(*o, core) for o in ring])
 
     first = here[0] * 2 + core
     for q in range(CHUNKS):
@@ -140,19 +142,25 @@
         return total
 
     def raw_first(d):
-        send(rt.at[pl.ds((d % 2) * HALF, HALF)], raw.at[d], wtx_sem.at[0], wrx_sem.at[0], next_to[d])
+        send(rt.at[pl.ds((d % 2) * HALF, HALF)], raw.at[d], wtx_sem, wrx_sem, next_to[d])
+
+    def raw_part(d, n):
+        rows = pl.ds((d % 2) * HALF + n * QUARTER, QUARTER)
+        send(rt.at[rows], raw.at[d, pl.ds(n * QUARTER, QUARTER)], wtx_sem, wrx_sem, next_to[d])
 
     def raw_second(d):
         rows = pl.ds((1 - d % 2) * HALF, QUARTER)
-        send(rt.at[rows], early.at[d], wtx_sem.at[1], wrx_sem.at[1], next_to[d])
+        send(rt.at[rows], early.at[d], etx_sem, erx_sem, next_to[d])
 
     def turn():
         for q in range(CHUNKS):
             rt[:, q * span:(q + 1) * span] = inp[q * span:(q + 1) * span].T
+        series = rt[...]
+        rt[...] = series - jnp.sum(series, axis=1, keepdims=True) / BARS
 
     @pl.when(core == 0)
     def _():
-        pl.semaphore_wait(barrier, len(zero_peers))
+        pl.semaphore_wait(barrier, 4 + 6)
         send(mrx.at[first], mrx.at[first], mtx_sem.at[0], mrx_sem.at[0], partner)
         for o in ring:
             send(mrx.at[first], mrx.at[first], mtx_sem.at[0], mrx_sem.at[0], away(*o, 1))
@@ -161,39 +169,42 @@
             raw_first(d)
         for d in range(6):
             raw_second(d)
-        drain(mrx.at[24], mrx_sem.at[2])
+        drain(mrx.at[pl.ds(8, 16)], mrx_sem.at[1])
         drain(mrx.at[pl.ds(0, 4)], mtx_sem.at[0])
 
     @pl.when(core == 1)
     def _():
-        pl.semaphore_wait(barrier, len(one_peers))
+        pl.semaphore_wait(barrier, 4 + 15 + 3 + 15)
         for o in ring:
             send(mrx.at[first], mrx.at[first], mtx_sem.at[0], mrx_sem.at[0], away(*o, 1))
         turn()
         for d in (2, 3, 4, 5):
-            raw_second(d)
+            raw_part(d, 0)
         for d in (0, 1):
             raw_first(d)
+        for d in (0, 1):
             raw_second(d)
         drain(mrx.at[pl.ds(0, 7)], mrx_sem.at[0])
         second = 8 + here[1] * 4 + here[2]
         mrx[second] = add_up(0, 8)
         for o in plane:
-            send(mrx.at[second], mrx.at[second], mtx_sem.at[1], mrx_sem.at[1], away(*o, 1))
+            for c in (0, 1):
+                send(mrx.at[second], mrx.at[second], mtx_sem.at[1], mrx_sem.at[1], away(*o, c))
+        send(mrx.at[second], mrx.at[second], mtx_sem.at[1], mrx_sem.at[1], partner)
         for d in (2, 3, 4, 5):
-            raw_first(d)
+            raw_part(d, 1)
+        for d in (2, 3, 4, 5):
+            raw_second(d)
         drain(mrx.at[pl.ds(8, 15)], mrx_sem.at[1])
-        mrx[24] = add_up(8, 16)
-        send(mrx.at[24], mrx.at[24], mtx_sem.at[2], mrx_sem.at[2], partner)
         drain(mrx.at[pl.ds(0, 3)], mtx_sem.at[0])
-        drain(mrx.at[pl.ds(8, 15)], mtx_sem.at[1])
-        drain(mrx.at[24], mtx_sem.at[2])
-
-    market = mrx[24] / (SER * 128)
+        drain(mrx.at[pl.ds(0, 15)], mtx_sem.at[1])
+        drain(mrx.at[pl.ds(0, 16)], mtx_sem.at[1])
+
+    market = add_up(8, 16) / (SER * 128)
+    swing = market - jnp.sum(market, axis=1, keepdims=True) / BARS
 
     def zscore(series):
-        excess = series - market
-        deviation = excess - jnp.sum(excess, axis=1, keepdims=True) / BARS
+        deviation = series - swing
         inverse = lax.rsqrt(
             jnp.sum(deviation * deviation, axis=1, keepdims=True) / BARS + 1e-6
         ) / math.sqrt(BARS)
@@ -218,7 +229,7 @@
                 )
     send(lhs.at[pl.ds(0, SER)], lhs.at[pl.ds(SER, SER)], ltx_sem, lrx_sem, partner)
 
-    drain(raw, wrx_sem.at[0])
+    drain(raw, wrx_sem)
     waiting = list(PLAN[0])
     for n in range(6):
         zbuf[2 + n] = zscore(raw[n])
@@ -229,7 +240,7 @@
             else:
                 forward(slot, d)
                 waiting.remove((slot, d))
-    drain(early, wrx_sem.at[1])
+    drain(early, erx_sem)
 
     def from_early(d, carry):
         zbuf[8 + d, :QUARTER] = zscore(early[d])
@@ -237,17 +248,21 @@
 
     lax.fori_loop(0, 6, from_early, 0)
 
-    def tiles(piece, sources, halves, where, send_sem, recv_sem):
+    def tiles(piece, origins, where, send_sem, recv_sem, side=None):
+        count = len(origins)
+        pieces = zbuf[pl.ds(piece, count)].reshape(count * HALF, BARS)
+        rows = slice(None) if side is None else slice(side * SER, (side + 1) * SER)
         both = lax.dot_general(
-            lhs[...], zbuf[pl.ds(piece, 2)].reshape(SER, BARS), (((1,), (1,)), ((), ())),
-            preferred_element_type=jnp.float32,
+            lhs[rows], pieces, (((1,), (1,)), ((), ())), preferred_element_type=jnp.float32
         )
-        for n in range(2):
+        for n, (source, half) in enumerate(origins):
             part = both[:, n * HALF:(n + 1) * HALF]
-            column = pl.ds(pl.multiple_of(sources[n] * SER + halves[n] * HALF, HALF), HALF)
-            where[n] = jnp.where(sources[n] >= theirs, part[SER:], 0.0).astype(jnp.bfloat16)
-            out_ref[:, column] = jnp.where(sources[n] >= mine, part[:SER], 0.0).astype(jnp.bfloat16)
-            send(where.at[n], out_ref.at[:, column], send_sem, recv_sem, partner)
+            column = pl.ds(pl.multiple_of(source * SER + half * HALF, HALF), HALF)
+            if side != 0:
+                where[n] = jnp.where(source >= theirs, part[-SER:], 0.0).astype(jnp.bfloat16)
+                send(where.at[n], out_ref.at[:, column], send_sem, recv_sem, partner)
+            if side != 1:
+                out_ref[:, column] = jnp.where(source >= mine, part[:SER], 0.0).astype(jnp.bfloat16)
 
     def landed(slot):
         if slot == 1:
@@ -255,9 +270,12 @@
         return zbuf.at[pl.ds(2 + 6 * slot, 6)]
 
     drain(lhs.at[pl.ds(SER, SER)], lrx_sem)
-    tiles(
-        0, (mine, mine), (0, 1), stage.at[2, pl.ds(0, 2)], ttx_sem.at[2], trx_sem.at[SLOTS]
-    )
+    tiles(0, ((mine, 0), (mine, 1)), stage.at[2, pl.ds(0, 2)], ttx_sem.at[2], trx_sem.at[SLOTS])
+
+    def settle(slot):
+        if slot:
+            drain(landed(slot), ztx_sem.at[slot])
+        drain(stage.at[0], trx_sem.at[slot])
 
     for slot in range(SLOTS):
         if slot:
@@ -267,34 +285,25 @@
         bank = slot % 2
         if slot >= 2:
             drain(stage.at[bank], ttx_sem.at[bank])
-        codes = [o[0] + 4 * o[1] + 16 * o[2] + 64 * h for _, o, h in TABLE[slot]]
-
-        def one(axis, carry, slot=slot, bank=bank, codes=codes):
-            sources, halves = [], []
-            for n in range(2):
-                code = jnp.where(axis == 0, codes[n], jnp.where(axis == 1, codes[2 + n], codes[4 + n]))
-                offset = (code % 4, code // 4 % 4, code // 16 % 4)
-                sources.append(block([(here[a] + 4 - offset[a]) % 4 for a in range(3)], core))
-                halves.append(code // 64)
+        origins = [
+            (block([(here[a] + 4 - o[a]) % 4 for a in range(3)], core), h) for _, o, h in TABLE[slot]
+        ]
+        for side in ((None,) if slot < SLOTS - 1 else (1, 0)):
             tiles(
-                2 + 6 * slot + 2 * axis, sources, halves, stage.at[bank, pl.ds(2 * axis, 2)],
-                ttx_sem.at[bank], trx_sem.at[slot],
+                2 + 6 * slot, origins, stage.at[bank], ttx_sem.at[bank], trx_sem.at[slot], side
             )
-            return carry
-
-        lax.fori_loop(0, 3, one, 0)
-
-    for slot in range(SLOTS):
-        if slot:
-            drain(landed(slot), ztx_sem.at[slot])
-        drain(stage.at[0], trx_sem.at[slot])
+        if slot >= BEHIND:
+            settle(slot - BEHIND)
+
+    for slot in range(SLOTS - BEHIND, SLOTS):
+        settle(slot)
     drain(stage.at[0], ttx_sem.at[0])
     drain(stage.at[1], ttx_sem.at[1])
     drain(stage.at[2, pl.ds(0, 2)], ttx_sem.at[2])
     drain(stage.at[2, pl.ds(0, 2)], trx_sem.at[SLOTS])
     drain(lhs.at[pl.ds(0, SER)], ltx_sem)
-    drain(raw, wtx_sem.at[0])
-    drain(early, wtx_sem.at[1])
+    drain(raw, wtx_sem)
+    drain(early, etx_sem)
 
 
 def write_out(held_ref, out_ref, sem):
@@ -323,8 +332,8 @@
             pltpu.VMEM((SER, BARS), jnp.float32),
             pltpu.VMEM((6, HALF, BARS), jnp.float32),
             pltpu.VMEM((6, QUARTER, BARS), jnp.float32),
-            pltpu.VMEM((25, 1, BARS), jnp.float32),
-            dma((CHUNKS,)), dma((3,)), dma((3,)), dma((2,)), dma((2,)), dma, dma,
+            pltpu.VMEM((24, 1, BARS), jnp.float32),
+            dma((CHUNKS,)), dma((2,)), dma((2,)), dma, dma, dma, dma, dma, dma,
             dma((SLOTS,)), dma((SLOTS,)), dma((3,)), dma((SLOTS + 1,)),
         ],
         compiler_params=pltpu.CompilerParams(

time: 84.8 us -> 83.5 us (0.985)
  Pallas kernels: 84.7 us -> 83.4 us
    pallas_call x1, Pallas kernels: 78.8 us -> 77.5 us  [shards(): pl.pallas_call(kernel, out_shape=pltpu.VMEM((SER, 128 * SER), jnp.bfloat1...]
where the time goes in v4:
time: 83.5 us; the launch traced here: 83.4 us
  Pallas kernels  83.4 us (100%)
    pallas_call x1, Pallas kernels, shards(): pl.pallas_call(kernel, out_shape=pltpu.VMEM((SER, 128 * SER), jnp.bfloat1...  77.5 us
    pallas_call x1, Pallas kernels, shards(): pl.pallas_call(write_out, out_shape=jax.ShapeDtypeStruct((SER, 128 * SER)...  5.92 us

profile of v4, /device:TPU:1, one launch (start us, length us, event | category | flops | bytes accessed | tf_op | source)
XLA Modules:
  0.0 83.4 jit_solution(3004197373045149551)
XLA Ops:
  0.0 77.5 %shard_map.17.held_ref = bf16[256,32768]{1,0:T(8,128)(2,1)S(1)} custom-call(f32[512,256]{1,0:T(8,128)} %r_ref.1), custom_call_target="tpu_custom_call" | custom-call | tf_op jit(solution)/shard_map/pallas_call | solution.py:322
  77.5 5.9 %shard_map.18 = bf16[256,32768]{1,0:T(8,128)(2,1)} custom-call(bf16[256,32768]{1,0:T(8,128)(2,1)S(1)} %shard_map.17.held_ref), custom_call_target="tpu_custom_call" | custom-call | tf_op jit(solution)/shard_map/pallas_call | solution.py:343

commit v5 on v4

--- a/solution.py
+++ b/solution.py
@@ -67,9 +67,8 @@
 
 
 def kernel(
-    r_ref, out_ref, zbuf, lhs, stage, inp, rt, raw, early, mrx,
-    in_sem, mtx_sem, mrx_sem, wtx_sem, wrx_sem, etx_sem, erx_sem,
-    ltx_sem, lrx_sem, ztx_sem, zrx_sem, ttx_sem, trx_sem,
+    r_ref, out_ref, zbuf, lhs, stage, inp, rt, raw, mrx,
+    met, in_sem, mtx_sem, mrx_sem, wtx_sem, wrx_sem, ltx_sem, lrx_sem, ztx_sem, zrx_sem, ttx_sem, trx_sem,
 ):
     span = BARS // CHUNKS
     loads = []
@@ -117,16 +116,17 @@
             pl.semaphore_signal(barrier, inc=1, device_id=to, device_id_type=MESH)
         return len(devices)
 
-    ring_peers = [partner] + [away(*o, 1 - core) for o in ring]
-    one_peers = [away(*o, 1) for o in plane]
+    around = [partner] + [away(*o, 1 - core) for o in ring]
+    axial = [away(*o, 1) for o in plane if 0 in o[1:]]
+    over_z = [away(*o, 1) for o in plane if o[1] == 0]
 
     @pl.when(core == 0)
     def _():
-        greet(ring_peers + next_to + one_peers)
+        greet(around + next_to + axial)
 
     @pl.when(core == 1)
     def _():
-        greet(ring_peers + one_peers + [away(*o, core) for o in ring])
+        greet(around + [away(*o, core) for o in ring] + axial)
 
     first = here[0] * 2 + core
     for q in range(CHUNKS):
@@ -143,14 +143,6 @@
 
     def raw_first(d):
         send(rt.at[pl.ds((d % 2) * HALF, HALF)], raw.at[d], wtx_sem, wrx_sem, next_to[d])
-
-    def raw_part(d, n):
-        rows = pl.ds((d % 2) * HALF + n * QUARTER, QUARTER)
-        send(rt.at[rows], raw.at[d, pl.ds(n * QUARTER, QUARTER)], wtx_sem, wrx_sem, next_to[d])
-
-    def raw_second(d):
-        rows = pl.ds((1 - d % 2) * HALF, QUARTER)
-        send(rt.at[rows], early.at[d], etx_sem, erx_sem, next_to[d])
 
     def turn():
         for q in range(CHUNKS):
@@ -167,34 +159,29 @@
         turn()
         for d in range(6):
             raw_first(d)
-        for d in range(6):
-            raw_second(d)
         drain(mrx.at[pl.ds(8, 16)], mrx_sem.at[1])
         drain(mrx.at[pl.ds(0, 4)], mtx_sem.at[0])
 
     @pl.when(core == 1)
     def _():
-        pl.semaphore_wait(barrier, 4 + 15 + 3 + 15)
+        pl.semaphore_wait(barrier, 4 + 3 + 6 + 6)
+        for to in over_z:
+            pl.semaphore_signal(met, inc=1, device_id=to, device_id_type=MESH)
         for o in ring:
             send(mrx.at[first], mrx.at[first], mtx_sem.at[0], mrx_sem.at[0], away(*o, 1))
         turn()
-        for d in (2, 3, 4, 5):
-            raw_part(d, 0)
         for d in (0, 1):
             raw_first(d)
-        for d in (0, 1):
-            raw_second(d)
         drain(mrx.at[pl.ds(0, 7)], mrx_sem.at[0])
         second = 8 + here[1] * 4 + here[2]
+        pl.semaphore_wait(met, 3)
         mrx[second] = add_up(0, 8)
         for o in plane:
             for c in (0, 1):
                 send(mrx.at[second], mrx.at[second], mtx_sem.at[1], mrx_sem.at[1], away(*o, c))
         send(mrx.at[second], mrx.at[second], mtx_sem.at[1], mrx_sem.at[1], partner)
         for d in (2, 3, 4, 5):
-            raw_part(d, 1)
-        for d in (2, 3, 4, 5):
-            raw_second(d)
+            raw_first(d)
         drain(mrx.at[pl.ds(8, 15)], mrx_sem.at[1])
         drain(mrx.at[pl.ds(0, 3)], mtx_sem.at[0])
         drain(mrx.at[pl.ds(0, 15)], mtx_sem.at[1])
@@ -216,7 +203,6 @@
             ztx_sem.at[slot], zrx_sem.at[slot], next_to[d],
         )
 
-    late = pl.ds(QUARTER, QUARTER)
     for half in range(2):
         z = zscore(rt[half * HALF:(half + 1) * HALF])
         zbuf[half] = z
@@ -224,7 +210,7 @@
         for d in range(6):
             if TABLE[1][d][0] == half:
                 send(
-                    zbuf.at[half, late], zbuf.at[8 + d, late],
+                    zbuf.at[half], zbuf.at[8 + d],
                     ztx_sem.at[1], zrx_sem.at[1], next_to[d],
                 )
     send(lhs.at[pl.ds(0, SER)], lhs.at[pl.ds(SER, SER)], ltx_sem, lrx_sem, partner)
@@ -240,14 +226,6 @@
             else:
                 forward(slot, d)
                 waiting.remove((slot, d))
-    drain(early, erx_sem)
-
-    def from_early(d, carry):
-        zbuf[8 + d, :QUARTER] = zscore(early[d])
-        return carry
-
-    lax.fori_loop(0, 6, from_early, 0)
-
     def tiles(piece, origins, where, send_sem, recv_sem, side=None):
         count = len(origins)
         pieces = zbuf[pl.ds(piece, count)].reshape(count * HALF, BARS)
@@ -265,8 +243,6 @@
                 out_ref[:, column] = jnp.where(source >= mine, part[:SER], 0.0).astype(jnp.bfloat16)
 
     def landed(slot):
-        if slot == 1:
-            return zbuf.at[pl.ds(8, 6), late]
         return zbuf.at[pl.ds(2 + 6 * slot, 6)]
 
     drain(lhs.at[pl.ds(SER, SER)], lrx_sem)
@@ -303,7 +279,6 @@
     drain(stage.at[2, pl.ds(0, 2)], trx_sem.at[SLOTS])
     drain(lhs.at[pl.ds(0, SER)], ltx_sem)
     drain(raw, wtx_sem)
-    drain(early, etx_sem)
 
 
 def write_out(held_ref, out_ref, sem):
@@ -331,9 +306,8 @@
             pltpu.VMEM((BARS, SER), jnp.float32),
             pltpu.VMEM((SER, BARS), jnp.float32),
             pltpu.VMEM((6, HALF, BARS), jnp.float32),
-            pltpu.VMEM((6, QUARTER, BARS), jnp.float32),
             pltpu.VMEM((24, 1, BARS), jnp.float32),
-            dma((CHUNKS,)), dma((2,)), dma((2,)), dma, dma, dma, dma, dma, dma,
+            pltpu.SemaphoreType.REGULAR, dma((CHUNKS,)), dma((2,)), dma((2,)), dma, dma, dma, dma,
             dma((SLOTS,)), dma((SLOTS,)), dma((3,)), dma((SLOTS + 1,)),
         ],
         compiler_params=pltpu.CompilerParams(

time: 83.5 us -> 83.2 us (level)
  no operation moved by 1% of the time
where the time goes in v5:
time: 83.2 us; the launch traced here: 83 us
  Pallas kernels  83 us (100%)
    pallas_call x1, Pallas kernels, shards(): pl.pallas_call(kernel, out_shape=pltpu.VMEM((SER, 128 * SER), jnp.bfloat1...  77.1 us
    pallas_call x1, Pallas kernels, shards(): pl.pallas_call(write_out, out_shape=jax.ShapeDtypeStruct((SER, 128 * SER)...  5.92 us

profile of v5, /device:TPU:1, one launch (start us, length us, event | category | flops | bytes accessed | tf_op | source)
XLA Modules:
  0.0 83.0 jit_solution(13213590963653543068)
XLA Ops:
  0.0 77.1 %shard_map.17.held_ref = bf16[256,32768]{1,0:T(8,128)(2,1)S(1)} custom-call(f32[512,256]{1,0:T(8,128)} %r_ref.1), custom_call_target="tpu_custom_call" | custom-call | tf_op jit(solution)/shard_map/pallas_call | solution.py:297
  77.1 5.9 %shard_map.18 = bf16[256,32768]{1,0:T(8,128)(2,1)} custom-call(bf16[256,32768]{1,0:T(8,128)(2,1)S(1)} %shard_map.17.held_ref), custom_call_target="tpu_custom_call" | custom-call | tf_op jit(solution)/shard_map/pallas_call | solution.py:317

commit v6 on v5

--- a/solution.py
+++ b/solution.py
@@ -19,13 +19,13 @@
 CHUNKS = 4
 
 TREE = [
-    [(0, 1), (0, 1), (0, 1)], [(0, -1), (0, -1), (0, -1)], [(1, 1), (1, -1), (4, -1)],
-    [(4, 1), (3, -1), (1, 1)], [(48, 1), (3, 1), (12, -1)], [(16, -1), (4, 1), (16, 1)],
-    [(17, 1), (16, -1), (3, -1)], [(32, -1), (16, 1), (8, 1)], [(13, 1), (15, -1), (17, 1)],
-    [(8, 1), (19, -1), (20, 1)], [(7, -1), (52, 1), (15, -1)], [(52, -1), (17, -1), (13, -1)],
-    [(49, 1), (17, 1), (7, 1)], [(52, 1), (18, -1), (28, 1)], [(24, -1), (35, 1), (61, -1)],
-    [(36, 1), (63, -1), (24, 1)], [(24, 1), (18, 1), (31, 1)], [(56, 1), (14, -1), (6, -1)],
-    [(61, 1), (39, 1), (18, 1)], [(59, -1), (45, -1), (22, 1)], [(43, -1), (30, -1), (30, 1)],
+    [(0, 1), (0, 1), (0, 1)], [(0, -1), (0, -1), (0, -1)], [(16, 1), (16, -1), (4, 1)],
+    [(48, 1), (1, 1), (12, -1)], [(4, -1), (4, 1), (3, -1)], [(1, 1), (48, 1), (48, -1)],
+    [(12, 1), (3, -1), (20, 1)], [(60, -1), (7, 1), (3, 1)], [(52, -1), (17, 1), (7, 1)],
+    [(51, -1), (49, -1), (8, 1)], [(17, 1), (19, -1), (5, -1)], [(28, 1), (2, -1), (51, -1)],
+    [(5, 1), (32, -1), (8, -1)], [(23, -1), (13, -1), (49, -1)], [(36, 1), (36, 1), (63, -1)],
+    [(63, -1), (61, -1), (55, -1)], [(24, -1), (21, 1), (50, -1)], [(40, -1), (14, -1), (11, -1)],
+    [(29, 1), (50, 1), (61, -1)], [(57, 1), (37, 1), (22, 1)], [(43, -1), (34, -1), (10, 1)],
 ]
 SLOTS = len(TREE)
 

time: 83.2 us -> 82.6 us (level)
  no operation moved by 1% of the time
where the time goes in v6:
time: 82.6 us; the launch traced here: 82.5 us
  Pallas kernels  82.5 us (100%)
    pallas_call x1, Pallas kernels, shards(): pl.pallas_call(kernel, out_shape=pltpu.VMEM((SER, 128 * SER), jnp.bfloat1...  76.6 us
    pallas_call x1, Pallas kernels, shards(): pl.pallas_call(write_out, out_shape=jax.ShapeDtypeStruct((SER, 128 * SER)...  5.92 us

profile of v6, /device:TPU:1, one launch (start us, length us, event | category | flops | bytes accessed | tf_op | source)
XLA Modules:
  0.0 82.5 jit_solution(12661993566213380265)
XLA Ops:
  0.0 76.6 %shard_map.17.held_ref = bf16[256,32768]{1,0:T(8,128)(2,1)S(1)} custom-call(f32[512,256]{1,0:T(8,128)} %r_ref.1), custom_call_target="tpu_custom_call" | custom-call | tf_op jit(solution)/shard_map/pallas_call | solution.py:297
  76.6 5.9 %shard_map.18 = bf16[256,32768]{1,0:T(8,128)(2,1)} custom-call(bf16[256,32768]{1,0:T(8,128)(2,1)S(1)} %shard_map.17.held_ref), custom_call_target="tpu_custom_call" | custom-call | tf_op jit(solution)/shard_map/pallas_call | solution.py:317

commit v7 on v6

--- a/solution.py
+++ b/solution.py
@@ -13,7 +13,7 @@
 SER = 256
 HALF = SER // 2
 PARTS = 8
-DEPTH = 4
+DEPTH = 6
 BEHIND = 3
 QUARTER = HALF // 2
 CHUNKS = 4
@@ -176,8 +176,8 @@
         second = 8 + here[1] * 4 + here[2]
         pl.semaphore_wait(met, 3)
         mrx[second] = add_up(0, 8)
-        for o in plane:
-            for c in (0, 1):
+        for c in (1, 0):
+            for o in plane:
                 send(mrx.at[second], mrx.at[second], mtx_sem.at[1], mrx_sem.at[1], away(*o, c))
         send(mrx.at[second], mrx.at[second], mtx_sem.at[1], mrx_sem.at[1], partner)
         for d in (2, 3, 4, 5):

time: 82.6 us -> 82.5 us (level)
  no operation moved by 1% of the time
where the time goes in v7:
time: 82.5 us; the launch traced here: 82.4 us
  Pallas kernels  82.4 us (100%)
    pallas_call x1, Pallas kernels, shards(): pl.pallas_call(kernel, out_shape=pltpu.VMEM((SER, 128 * SER), jnp.bfloat1...  76.5 us
    pallas_call x1, Pallas kernels, shards(): pl.pallas_call(write_out, out_shape=jax.ShapeDtypeStruct((SER, 128 * SER)...  5.92 us

profile of v7, /device:TPU:1, one launch (start us, length us, event | category | flops | bytes accessed | tf_op | source)
XLA Modules:
  0.0 82.4 jit_solution(18160255247703835295)
XLA Ops:
  0.0 76.5 %shard_map.17.held_ref = bf16[256,32768]{1,0:T(8,128)(2,1)S(1)} custom-call(f32[512,256]{1,0:T(8,128)} %r_ref.1), custom_call_target="tpu_custom_call" | custom-call | tf_op jit(solution)/shard_map/pallas_call | solution.py:297
  76.5 5.9 %shard_map.18 = bf16[256,32768]{1,0:T(8,128)(2,1)} custom-call(bf16[256,32768]{1,0:T(8,128)(2,1)S(1)} %shard_map.17.held_ref), custom_call_target="tpu_custom_call" | custom-call | tf_op jit(solution)/shard_map/pallas_call | solution.py:317
